TPU v7x, 512 devices: a whole 4x8x8 slice. The times are simulated.
512 devices in a mesh: dp: 16 (over z, y_lo), comp: 32 (over y_hi, x, core).
Axes of the slice: x: 4, y: 8 (y_hi: 4, y_lo: 2; y = y_hi * 2 + y_lo), z: 8, core: 2. Of those that a mesh axis runs over, the one named last changes fastest.
Arguments:
- vectors: bfloat16 [2048, 256], P('dp'), may hold values from -8 to 8
- centers: float32 [512, 256], P('comp'), may hold values from -1.5 to 1.5
- factors: bfloat16 [512, 256, 256], P('comp', 'dp'), may hold values from -1 to 9.065873, as said below
- mixing: float32 [512], P('comp'), may hold values from 0.0005859375 to 0.005859375
Outputs:
- new_factors: float32 [512, 256, 256], P('comp', 'dp')
- new_means: float32 [512, 256], P('comp')
- new_weights: float32 [512], P('comp')
- evidence: float32 [2048], P('dp')
Inputs may be any that keep to these rules, and one draw needn't show every extreme that they name: `factors`: each component's 256 x 256 factor is lower triangular with a positive diagonal.
All inputs are finite; a program needn't handle non-finite values.
Results may differ from a plain program's by a relative error of at most 0.0003.
Values may be sent and summed in bfloat16 or wider, within the bound.
No kernel may reach another device: no remote copies, remote signals or barrier semaphores. Data moves between devices by JAX's collectives and lax.ppermute only.
A program may use at most 64 MiB of HBM per device.

v0:
```python
import math
import jax
import jax.numpy as jnp
from jax import lax
from jax.sharding import PartitionSpec as P

anneal = 1.0
step_weight = 0.5
ridge_term = 0.01
normal_offset = 0.9189385332046727
exact_mode = lax.Precision.HIGHEST


def sent_to_all(shard, axis):
    copies = jnp.broadcast_to(shard, (lax.axis_size(axis), *shard.shape))
    return lax.all_to_all(copies, axis, split_axis=0, concat_axis=0, tiled=True)


def of_everyone(shard, axis):
    everything = sent_to_all(shard, axis)
    return jnp.max(everything, axis=0)


def taken_together(shard, axis):
    return sent_to_all(shard, axis).sum(axis=0)


def in_order(tiles, dim):
    lengths = list(tiles.shape[1:])
    lengths[dim] *= tiles.shape[0]
    return jnp.moveaxis(tiles, 0, dim).reshape(lengths)


def gather_directly(shard, axis, dim):
    tiles = sent_to_all(shard, axis)
    return in_order(tiles, dim)


def in_blocks(shard, dim, peers):
    lengths = shard.shape
    tiles = shard.reshape(*lengths[:dim], peers, lengths[dim] // peers, *lengths[dim + 1 :])
    return jnp.moveaxis(tiles, dim, 0)


def summed_on_arrival(shard, axis, dim):
    tiles = in_blocks(shard, dim, lax.axis_size(axis))
    arrived = lax.all_to_all(tiles, axis, split_axis=0, concat_axis=0, tiled=True)
    return arrived.sum(axis=0)


def normalize(density, mixing, features):
    scores = anneal * (density + jnp.log(mixing)[:, None] - features * normal_offset)
    row_max = jnp.max(scores, axis=0)
    joined_max = of_everyone(row_max, "comp")
    joined_total = taken_together(jnp.sum(jnp.exp(scores - joined_max[None, :]), axis=0), "comp")
    shares = jnp.exp(scores - joined_max[None, :]) / joined_total[None, :]
    evidence = (joined_max + jnp.log(joined_total)) / anneal
    return (shares, evidence)


def refactor(pieces):
    scaled, moment_part = pieces
    identity = jnp.eye(scaled.shape[-1], dtype=jnp.float32)
    inverse = lax.linalg.triangular_solve(scaled, identity, left_side=True, lower=True)
    covariance = (
        jnp.dot(inverse, inverse.T, precision=exact_mode) + moment_part + ridge_term * identity
    )
    cholesky_factor = jnp.linalg.cholesky(covariance)
    return lax.linalg.triangular_solve(cholesky_factor, identity, left_side=True, lower=True)


def local(vectors, centers, factors, mixing):
    comp_count, row_count, features = factors.shape
    groups = lax.axis_size("dp")
    owned_count = comp_count // groups
    position = lax.axis_index("dp")
    row_start = position * row_count
    everyone = gather_directly(vectors, "dp", 0)
    vector_total = everyone.shape[0]
    block_rows = math.gcd(vector_total, 512)
    block_count = vector_total // block_rows
    shifted = jnp.einsum("krd,kd->kr", factors.astype(jnp.float32), centers, precision=exact_mode)
    diag_block = lax.dynamic_slice_in_dim(factors, row_start, row_count, 2).astype(jnp.float32)
    log_diag = jnp.sum(jnp.log(jnp.diagonal(diag_block, axis1=1, axis2=2)), axis=1)
    flattened = factors.reshape(comp_count * row_count, features)
    vector_blocks = everyone.reshape(block_count, block_rows, features)

    def density_block(vector_block):
        whitened = lax.dot_general(
            flattened, vector_block, (((1,), (1,)), ((), ())), preferred_element_type=jnp.float32
        )
        whitened = whitened.reshape(comp_count, row_count, -1) - shifted[:, :, None]
        return log_diag[:, None] - 0.5 * jnp.sum(whitened * whitened, axis=1)

    partial_density = (
        lax.map(density_block, vector_blocks).transpose(1, 0, 2).reshape(comp_count, vector_total)
    )
    density = summed_on_arrival(partial_density, "dp", 1)
    shares_local, evidence = normalize(density, mixing, features)
    shares_all = gather_directly(shares_local, "dp", 1)
    share_blocks = shares_all.reshape(comp_count, block_count, block_rows).transpose(1, 0, 2)

    def accumulate(running, inputs):
        first_sum, gram_sum = running
        vector_block, share_block = inputs
        wide_block = vector_block.astype(jnp.float32)
        first_sum = first_sum + jnp.dot(share_block, wide_block, precision=exact_mode)
        own_share = lax.dynamic_slice_in_dim(share_block, position * owned_count, owned_count, 0)
        weighted = own_share[:, None, :] * wide_block.T[None]
        weighted = weighted.reshape(owned_count * features, -1)
        gram_term = jnp.dot(weighted, wide_block, precision=exact_mode)
        return ((first_sum, gram_sum + gram_term), None)

    gram_start = jnp.zeros((owned_count * features, features), jnp.float32)
    first_start = jnp.zeros((comp_count, features), jnp.float32)
    (first_moment, gram_sum), unused = lax.scan(
        accumulate, (first_start, gram_start), (vector_blocks, share_blocks)
    )
    counts = jnp.sum(shares_all, axis=1)
    kept_share = (1.0 - step_weight) * mixing
    new_weights = kept_share + step_weight * counts / vector_total
    new_means = (
        kept_share[:, None] * centers + step_weight * first_moment / vector_total
    ) / new_weights[:, None]
    retained = kept_share / new_weights
    own_start = position * owned_count
    kept_own = lax.dynamic_slice_in_dim(kept_share, own_start, owned_count, 0)
    weight_own = lax.dynamic_slice_in_dim(new_weights, own_start, owned_count, 0)
    retained_own = lax.dynamic_slice_in_dim(retained, own_start, owned_count, 0)
    center_own = lax.dynamic_slice_in_dim(centers, own_start, owned_count, 0)
    mean_own = lax.dynamic_slice_in_dim(new_means, own_start, owned_count, 0)
    gram_own = gram_sum.reshape(owned_count, features, features)
    moment_part = (
        kept_own[:, None, None] * center_own[:, :, None] * center_own[:, None, :]
        + step_weight * gram_own / vector_total
    ) / weight_own[:, None, None] - mean_own[:, :, None] * mean_own[:, None, :]
    whole_factors = lax.all_to_all(
        factors.reshape(groups, owned_count, row_count, features),
        "dp",
        split_axis=0,
        concat_axis=2,
        tiled=True,
    )
    scaled = whole_factors[0].astype(jnp.float32) * lax.rsqrt(retained_own)[:, None, None]
    refreshed = lax.map(refactor, (scaled, moment_part))
    new_factors = lax.all_to_all(
        refreshed[None], "dp", split_axis=2, concat_axis=0, tiled=True
    ).reshape(comp_count, row_count, features)
    return (new_factors, new_means, new_weights, evidence)


def solution(mesh):
    return jax.shard_map(
        local,
        mesh=mesh,
        in_specs=(P("dp", None), P("comp", None), P("comp", "dp", None), P("comp")),
        out_specs=(P("comp", "dp", None), P("comp", None), P("comp"), P("dp")),
        check_vma=False,
    )
```

profile of v0, /device:TPU:8, one launch (start us, length us, event | category | flops | bytes accessed | tf_op | source)
XLA Modules:
  0.0 226.2 jit_solution(829906853297270123)
XLA Ops:
  0.6 1.9 broadcast_in_dim.32
  2.6 11.8 %all-to-all-start.1 = ((bf16[16,128,256]{2,1,0:T(8,128)(2,1)}), bf16[16,128,256]{2,1,0:T(8,128)(2,1)S(1)}, u32[]{:S(2)}, u32[]{:S(2)}) async-start(bf16[16,128,256]{2,1,0:T(8,128)(2,1)} %broadcast_in_dim.32), calls=%async_computation.1 | async-start | bytes 2097152 | tf_op jit(solution)/shard_map/all_to_all | solution.py:16
  16.2 1.1 fusion.33
  17.3 24.4 %all-to-all-done.1 = bf16[16,128,256]{2,1,0:T(8,128)(2,1)S(1)} async-done(((bf16[16,128,256]{2,1,0:T(8,128)(2,1)}), bf16[16,128,256]{2,1,0:T(8,128)(2,1)S(1)}, u32[]{:S(2)}, u32[]{:S(2)}) %all-to-all-start.1) | async-done | bytes 1048608 | tf_op jit(solution)/shard_map/all_to_all | solution.py:16
  41.7 5.2 %while.34 = (s32[]{:T(128)}, f32[4,16,512]{2,1,0:T(8,128)S(1)}, f32[16]{0:T(128)S(1)}, bf16[4,512,256]{2,1,0:T(8,128)(2,1)S(1)}, bf16[256,256]{1,0:T(8,128)(2,1)}, /*index=5*/f32[16,16]{1,0:T(8,128)S(1)}, s32[]{:T(128)}) while((s32[]{:T(128)}, f32[4,16,512]{2,1,0:T(8,128)S(1)}, f32[16]{0:T(128)S(1)}, bf16[4,512,256]{2,1,0:T(8,128)(2,1)S(1)}, ...), condition=%wide.region_3.4_spmd, body=%wide.region_1.3_spmd.sunk | while | flops 67510272 | bytes 500309 | solution.py:96
  41.7 1.2 multiply_reduce_fusion.2
  43.0 1.2 multiply_reduce_fusion.2
  44.3 1.2 multiply_reduce_fusion.2
  45.6 1.2 multiply_reduce_fusion.2
  47.7 4.5 %all-to-all-start.2 = ((f32[16,16,128]{2,1,0:T(8,128)}), f32[16,16,128]{2,1,0:T(8,128)S(1)}, u32[]{:S(2)}, u32[]{:S(2)}) async-start(f32[16,16,128]{2,1,0:T(8,128)} %copy.58), calls=%async_computation.2 | async-start | bytes 262144 | tf_op jit(solution)/shard_map/all_to_all | solution.py:47
  52.2 8.5 %all-to-all-done.2 = f32[16,16,128]{2,1,0:T(8,128)S(1)} async-done(((f32[16,16,128]{2,1,0:T(8,128)}), f32[16,16,128]{2,1,0:T(8,128)S(1)}, u32[]{:S(2)}, u32[]{:S(2)}) %all-to-all-start.2) | async-done | bytes 131104 | tf_op jit(solution)/shard_map/all_to_all | solution.py:47
  60.8 18.6 %all_to_all.45 = f32[32,1,128]{2,1,0:T(1,128)S(1)} all-to-all(f32[32,1,128]{2,1,0:T(1,128)S(1)} %broadcast_in_dim.33), channel_id=1, replica_groups=mesh['dp'=16,'comp'=32] {'comp'}, dimensions={0} | all-to-all | bytes 32768 | tf_op jit(solution)/shard_map/all_to_all | solution.py:16
  79.6 12.8 %all_to_all.46 = f32[32,1,128]{2,1,0:T(1,128)S(1)} all-to-all(f32[32,1,128]{2,1,0:T(1,128)S(1)} %broadcast_in_dim.34), channel_id=1, replica_groups=mesh['dp'=16,'comp'=32] {'comp'}, dimensions={0} | all-to-all | bytes 32768 | tf_op jit(solution)/shard_map/all_to_all | solution.py:16
  93.1 4.0 %all-to-all-start.5 = ((f32[16,16,128]{2,1,0:T(8,128)}), f32[16,16,128]{2,1,0:T(8,128)S(1)}, u32[]{:S(2)}, u32[]{:S(2)}) async-start(f32[16,16,128]{2,1,0:T(8,128)} %broadcast_in_dim.35), calls=%async_computation.5 | async-start | bytes 262144 | tf_op jit(solution)/shard_map/all_to_all | solution.py:16
  97.2 8.5 %all-to-all-done.5 = f32[16,16,128]{2,1,0:T(8,128)S(1)} async-done(((f32[16,16,128]{2,1,0:T(8,128)}), f32[16,16,128]{2,1,0:T(8,128)S(1)}, u32[]{:S(2)}, u32[]{:S(2)}) %all-to-all-start.5) | async-done | bytes 131104 | tf_op jit(solution)/shard_map/all_to_all | solution.py:16
  105.7 4.3 %all-to-all-start = ((bf16[16,1,16,256]{3,2,1,0:T(8,128)(2,1)}), bf16[16,1,16,256]{3,2,1,0:T(8,128)(2,1)S(1)}, u32[]{:S(2)}, u32[]{:S(2)}) async-start(bf16[16,1,16,256]{3,2,1,0:T(8,128)(2,1)} %bitcast.4), calls=%async_computation | async-start | bytes 262144 | tf_op jit(solution)/shard_map/all_to_all | solution.py:137
  110.1 3.8 %while.35 = (s32[]{:T(128)}, f32[16,256]{1,0:T(8,128)S(1)}, f32[256,256]{1,0:T(8,128)S(1)}, f32[4,16,512]{2,1,0:T(8,128)S(1)}, bf16[4,512,256]{2,1,0:T(8,128)(2,...) while((s32[]{:T(128)}, f32[16,256]{1,0:T(8,128)S(1)}, f32[256,256]{1,0:T(8,128)S(1)}, ...), condition=%wide.region_11.13_spmd.clone, body=%wide.region_10.12_spmd.clone.sunk | while | flops 428220416 | bytes 1384576 | solution.py:116
  116.9 1.5 all-to-all-done
  118.6 4.0 %while.36 = (s32[]{:T(128)}, f32[256,256]{1,0:T(8,128)S(1)}, s32[2,2]{1,0:T(2,128)S(1)}, f32[2,128,128]{2,1,0:T(8,128)S(1)}, s32[]{:T(128)}) while((s32[]{:T(128)}, f32[256,256]{1,0:T(8,128)S(1)}, s32[2,2]{1,0:T(2,128)S(1)}, f32[2,128,128]{2,1,0:T(8,128)S(1)}, s32[]{:T(128)}) %tuple.98), condition=%wide.while_cond, body=%wide.while_body.sunk | while | flops 2 | bytes 131181 | solution.py:64
  119.2 1.4 bitcast_dynamic-update-slice_fusion.4
  121.2 1.4 bitcast_dynamic-update-slice_fusion.4
  122.6 19.9 %custom-call.23 = f32[2,128,128]{1,2,0:T(8,128)S(1)} custom-call(f32[2,128,128]{2,1,0:T(8,128)S(1)} %get-tuple-element.199), custom_call_target="InvertDiagBlocksLowerTriangular" | custom-call | tf_op jit(solution)/shard_map/while/body/eval_jaxpr/triangular_solve/custom-call.0 | solution.py:64
  144.1 1.1 fusion.16
  145.4 11.7 %cholesky.49 = f32[128,128]{1,0:T(8,128)S(1)} custom-call(f32[128,128]{1,0:T(8,128)S(1)} %cholesky.115), custom_call_target="Cholesky" | custom-call | tf_op jit(solution)/shard_map/while/body/eval_jaxpr/jit(cholesky)/cholesky | solution.py:68
  157.1 9.8 %custom-call.17 = f32[1,128,128]{1,2,0:T(8,128)S(1)} custom-call(f32[1,128,128]{2,1,0:T(8,128)S(1)} %get-tuple-element.292), custom_call_target="InvertDiagBlocksLowerTriangular" | custom-call | tf_op jit(solution)/shard_map/while/body/eval_jaxpr/jit(cholesky)/cholesky | solution.py:68
  167.4 11.7 %cholesky.103 = f32[128,128]{1,0:T(8,128)S(1)} custom-call(f32[128,128]{1,0:T(8,128)S(1)} %convolution_subtract_fusion.2), custom_call_target="Cholesky" | custom-call | tf_op jit(solution)/shard_map/while/body/eval_jaxpr/jit(cholesky)/cholesky | solution.py:68
  182.3 4.3 %while.37 = (s32[]{:T(128)}, f32[256,256]{0,1:T(8,128)S(1)}, s32[2,2]{1,0:T(2,128)S(1)}, f32[2,128,128]{2,1,0:T(8,128)S(1)}, s32[]{:T(128)}) while((s32[]{:T(128)}, f32[256,256]{0,1:T(8,128)S(1)}, s32[2,2]{1,0:T(2,128)S(1)}, f32[2,128,128]{2,1,0:T(8,128)S(1)}, s32[]{:T(128)}) %tuple.110), condition=%wide.while_cond.clone, body=%wide.while_body.clone.sunk | while | flops 2 | bytes 393321 | solution.py:69
  182.9 1.4 dynamic-slice.21
  185.1 1.4 dynamic-slice.21
  186.6 19.9 %custom-call.24 = f32[2,128,128]{1,2,0:T(8,128)S(1)} custom-call(f32[2,128,128]{2,1,0:T(8,128)S(1)} %get-tuple-element.200), custom_call_target="InvertDiagBlocksLowerTriangular" | custom-call | tf_op jit(solution)/shard_map/while/body/eval_jaxpr/triangular_solve/custom-call.0 | solution.py:69
  208.6 7.2 %all-to-all-start.6 = ((f32[1,1,256,256]{3,1,0,2:T(1,128)}), f32[1,1,256,256]{3,1,0,2:T(1,128)S(1)}, u32[]{:S(2)}, u32[]{:S(2)}) async-start(f32[1,1,256,256]{3,1,0,2:T(1,128)} %copy.72), calls=%async_computation.6 | async-start | bytes 524288 | tf_op jit(solution)/shard_map/all_to_all | solution.py:146
  216.3 9.2 %all-to-all-done.6 = f32[1,1,256,256]{3,1,0,2:T(1,128)S(1)} async-done(((f32[1,1,256,256]{3,1,0,2:T(1,128)}), f32[1,1,256,256]{3,1,0,2:T(1,128)S(1)}, u32[]{:S(2)}, u32[]{:S(2)}) %all-to-all-start.6) | async-done | bytes 262176 | tf_op jit(solution)/shard_map/all_to_all | solution.py:146
  (103 shorter events, 20.0 us)
Async XLA Ops:
  2.6 39.1 %all-to-all-start.1 = ((bf16[16,128,256]{2,1,0:T(8,128)(2,1)}), bf16[16,128,256]{2,1,0:T(8,128)(2,1)S(1)}, u32[]{:S(2)}, u32[]{:S(2)}) async-start(bf16[16,128,256]{2,1,0:T(8,128)(2,1)} %broadcast_in_dim.32), calls=%async_computation.1 | async-start | bytes 2097152 | tf_op jit(solution)/shard_map/all_to_all | solution.py:16
  15.5 0.7 copy-start
  47.7 4.5 %copy-start.3 = (f32[16]{0:T(128)S(1)}, f32[16]{0:T(128)}, u32[]{:S(2)}) copy-start(f32[16]{0:T(128)} %param.13) | copy-start | bytes 196
  47.7 13.0 %all-to-all-start.2 = ((f32[16,16,128]{2,1,0:T(8,128)}), f32[16,16,128]{2,1,0:T(8,128)S(1)}, u32[]{:S(2)}, u32[]{:S(2)}) async-start(f32[16,16,128]{2,1,0:T(8,128)} %copy.58), calls=%async_computation.2 | async-start | bytes 262144 | tf_op jit(solution)/shard_map/all_to_all | solution.py:47
  93.1 12.6 %all-to-all-start.5 = ((f32[16,16,128]{2,1,0:T(8,128)}), f32[16,16,128]{2,1,0:T(8,128)S(1)}, u32[]{:S(2)}, u32[]{:S(2)}) async-start(f32[16,16,128]{2,1,0:T(8,128)} %broadcast_in_dim.35), calls=%async_computation.5 | async-start | bytes 262144 | tf_op jit(solution)/shard_map/all_to_all | solution.py:16
  105.7 12.7 %all-to-all-start = ((bf16[16,1,16,256]{3,2,1,0:T(8,128)(2,1)}), bf16[16,1,16,256]{3,2,1,0:T(8,128)(2,1)S(1)}, u32[]{:S(2)}, u32[]{:S(2)}) async-start(bf16[16,1,16,256]{3,2,1,0:T(8,128)(2,1)} %bitcast.4), calls=%async_computation | async-start | bytes 262144 | tf_op jit(solution)/shard_map/all_to_all | solution.py:137
  114.2 2.7 %copy-start.2 = (f32[16]{0:T(128)}, f32[16]{0:T(128)S(1)}, u32[]{:S(2)}) copy-start(f32[16]{0:T(128)S(1)} %get-tuple-element.286) | copy-start | bytes 196
  116.9 1.6 copy-start.1
  208.6 16.9 %all-to-all-start.6 = ((f32[1,1,256,256]{3,1,0,2:T(1,128)}), f32[1,1,256,256]{3,1,0,2:T(1,128)S(1)}, u32[]{:S(2)}, u32[]{:S(2)}) async-start(f32[1,1,256,256]{3,1,0,2:T(1,128)} %copy.72), calls=%async_computation.6 | async-start | bytes 524288 | tf_op jit(solution)/shard_map/all_to_all | solution.py:146
where the time goes:
time: 227 us; the launch traced here: 226 us
  other arithmetic  76.6 us (34%)
  waiting for transfers between devices  52.1 us (23%)
  starting transfers between devices  31.7 us (14%)
  blocking collectives  31.4 us (14%)
  local copies, waits for them, and re-layouts  17.9 us (8%)
  matrix products  13.1 us (6%)
  between operations  3.05 us (1%)
    another operation x7, other arithmetic, refactor(): cholesky_factor = jnp.linalg.cholesky(covariance)  34.7 us
    all_to_all x2, waiting for transfers between devices, sent_to_all(): return lax.all_to_all(copies, axis, split_axis=0, concat_axis=0, tiled=True)  32.9 us
    all_to_all x2, blocking collectives, sent_to_all(): return lax.all_to_all(copies, axis, split_axis=0, concat_axis=0, tiled=True)  31.4 us
    another operation x2, other arithmetic, refactor(): lax.linalg.triangular_solve(cholesky_factor, identity, left_side=True, lo...  19.9 us
    another operation x3, other arithmetic, refactor(): lax.linalg.triangular_solve(scaled, identity, left_side=True, lower=True)  19.9 us
    all_to_all x2, starting transfers between devices, sent_to_all(): return lax.all_to_all(copies, axis, split_axis=0, concat_axis=0, tiled=True)  15.8 us
    all_to_all x1, waiting for transfers between devices, local(): lax.all_to_all(refreshed[None], 'dp', split_axis=2, concat_axis=0, tiled=...  9.18 us
    all_to_all x1, waiting for transfers between devices, summed_on_arrival(): lax.all_to_all(tiles, axis, split_axis=0, concat_axis=0, tiled=True)  8.49 us
  transfers between devices with their start and end apart: 5, of which 5 were waited for; matrix products, arithmetic and copies ran while one was open for 4% of the time, Pallas kernels for 0%

commit v1 on v0

--- a/solution.py
+++ b/solution.py
@@ -143,8 +143,11 @@
     )
     scaled = whole_factors[0].astype(jnp.float32) * lax.rsqrt(retained_own)[:, None, None]
     refreshed = lax.map(refactor, (scaled, moment_part))
-    new_factors = lax.all_to_all(
-        refreshed[None], "dp", split_axis=2, concat_axis=0, tiled=True
+    new_factors = jnp.concatenate(
+        lax.all_to_all(
+            jnp.stack(jnp.split(refreshed[None], lax.axis_size("dp"), axis=2)), "dp", 0, 0
+        ),
+        axis=0,
     ).reshape(comp_count, row_count, features)
     return (new_factors, new_means, new_weights, evidence)
 

time: 227 us -> 236 us (1.040)
  local copies, waits for them, and re-layouts: 17.9 us -> 26.6 us
    unnamed x11 -> x26, local copies, waits for them, and re-layouts: 0.98 us -> 10.1 us
where the time goes in v1:
time: 236 us; the launch traced here: 235 us
  other arithmetic  76.6 us (32%)
  waiting for transfers between devices  52.1 us (22%)
  starting transfers between devices  31.7 us (13%)
  blocking collectives  31.4 us (13%)
  local copies, waits for them, and re-layouts  26.6 us (11%)
  matrix products  13.1 us (6%)
  between operations  3.06 us (1%)
    another operation x7, other arithmetic, refactor(): cholesky_factor = jnp.linalg.cholesky(covariance)  34.7 us
    all_to_all x2, waiting for transfers between devices, sent_to_all(): return lax.all_to_all(copies, axis, split_axis=0, concat_axis=0, tiled=True)  32.9 us
    all_to_all x2, blocking collectives, sent_to_all(): return lax.all_to_all(copies, axis, split_axis=0, concat_axis=0, tiled=True)  31.4 us
    another operation x2, other arithmetic, refactor(): lax.linalg.triangular_solve(cholesky_factor, identity, left_side=True, lo...  19.9 us
    another operation x3, other arithmetic, refactor(): lax.linalg.triangular_solve(scaled, identity, left_side=True, lower=True)  19.9 us
    all_to_all x2, starting transfers between devices, sent_to_all(): return lax.all_to_all(copies, axis, split_axis=0, concat_axis=0, tiled=True)  15.8 us
    unnamed x26, local copies, waits for them, and re-layouts  10.1 us
    all_to_all x1, waiting for transfers between devices, local(): lax.all_to_all(jnp.stack(jnp.split(refreshed[None], lax.axis_size('dp'),...  9.18 us
  transfers between devices with their start and end apart: 5, of which 5 were waited for; matrix products, arithmetic and copies ran while one was open for 4% of the time, Pallas kernels for 0%

profile of v1, /device:TPU:8, one launch (start us, length us, event | category | flops | bytes accessed | tf_op | source)
XLA Modules:
  0.0 234.9 jit_solution(7811785068693116390)
XLA Ops:
  0.6 1.9 broadcast_in_dim.32
  2.6 11.8 %all-to-all-start.1 = ((bf16[16,128,256]{2,1,0:T(8,128)(2,1)}), bf16[16,128,256]{2,1,0:T(8,128)(2,1)S(1)}, u32[]{:S(2)}, u32[]{:S(2)}) async-start(bf16[16,128,256]{2,1,0:T(8,128)(2,1)} %broadcast_in_dim.32), calls=%async_computation.1 | async-start | bytes 2097152 | tf_op jit(solution)/shard_map/all_to_all | solution.py:16
  16.2 1.1 fusion.33
  17.3 24.4 %all-to-all-done.1 = bf16[16,128,256]{2,1,0:T(8,128)(2,1)S(1)} async-done(((bf16[16,128,256]{2,1,0:T(8,128)(2,1)}), bf16[16,128,256]{2,1,0:T(8,128)(2,1)S(1)}, u32[]{:S(2)}, u32[]{:S(2)}) %all-to-all-start.1) | async-done | bytes 1048608 | tf_op jit(solution)/shard_map/all_to_all | solution.py:16
  41.7 5.2 %while.34 = (s32[]{:T(128)}, f32[4,16,512]{2,1,0:T(8,128)S(1)}, f32[16]{0:T(128)S(1)}, bf16[4,512,256]{2,1,0:T(8,128)(2,1)S(1)}, bf16[256,256]{1,0:T(8,128)(2,1)}, /*index=5*/f32[16,16]{1,0:T(8,128)S(1)}, s32[]{:T(128)}) while((s32[]{:T(128)}, f32[4,16,512]{2,1,0:T(8,128)S(1)}, f32[16]{0:T(128)S(1)}, bf16[4,512,256]{2,1,0:T(8,128)(2,1)S(1)}, ...), condition=%wide.region_3.4_spmd, body=%wide.region_1.3_spmd.sunk | while | flops 67510272 | bytes 500309 | solution.py:96
  41.7 1.2 multiply_reduce_fusion.2
  43.0 1.2 multiply_reduce_fusion.2
  44.3 1.2 multiply_reduce_fusion.2
  45.6 1.2 multiply_reduce_fusion.2
  47.7 4.5 %all-to-all-start.2 = ((f32[16,16,128]{2,1,0:T(8,128)}), f32[16,16,128]{2,1,0:T(8,128)S(1)}, u32[]{:S(2)}, u32[]{:S(2)}) async-start(f32[16,16,128]{2,1,0:T(8,128)} %copy.56), calls=%async_computation.2 | async-start | bytes 262144 | tf_op jit(solution)/shard_map/all_to_all | solution.py:47
  52.2 8.5 %all-to-all-done.2 = f32[16,16,128]{2,1,0:T(8,128)S(1)} async-done(((f32[16,16,128]{2,1,0:T(8,128)}), f32[16,16,128]{2,1,0:T(8,128)S(1)}, u32[]{:S(2)}, u32[]{:S(2)}) %all-to-all-start.2) | async-done | bytes 131104 | tf_op jit(solution)/shard_map/all_to_all | solution.py:47
  60.8 18.6 %all_to_all.41 = f32[32,1,128]{2,1,0:T(1,128)S(1)} all-to-all(f32[32,1,128]{2,1,0:T(1,128)S(1)} %broadcast_in_dim.33), channel_id=1, replica_groups=mesh['dp'=16,'comp'=32] {'comp'}, dimensions={0} | all-to-all | bytes 32768 | tf_op jit(solution)/shard_map/all_to_all | solution.py:16
  79.6 12.8 %all_to_all.42 = f32[32,1,128]{2,1,0:T(1,128)S(1)} all-to-all(f32[32,1,128]{2,1,0:T(1,128)S(1)} %broadcast_in_dim.34), channel_id=1, replica_groups=mesh['dp'=16,'comp'=32] {'comp'}, dimensions={0} | all-to-all | bytes 32768 | tf_op jit(solution)/shard_map/all_to_all | solution.py:16
  93.1 4.0 %all-to-all-start.5 = ((f32[16,16,128]{2,1,0:T(8,128)}), f32[16,16,128]{2,1,0:T(8,128)S(1)}, u32[]{:S(2)}, u32[]{:S(2)}) async-start(f32[16,16,128]{2,1,0:T(8,128)} %broadcast_in_dim.35), calls=%async_computation.5 | async-start | bytes 262144 | tf_op jit(solution)/shard_map/all_to_all | solution.py:16
  97.2 8.5 %all-to-all-done.5 = f32[16,16,128]{2,1,0:T(8,128)S(1)} async-done(((f32[16,16,128]{2,1,0:T(8,128)}), f32[16,16,128]{2,1,0:T(8,128)S(1)}, u32[]{:S(2)}, u32[]{:S(2)}) %all-to-all-start.5) | async-done | bytes 131104 | tf_op jit(solution)/shard_map/all_to_all | solution.py:16
  105.7 4.3 %all-to-all-start = ((bf16[16,1,16,256]{3,2,1,0:T(8,128)(2,1)}), bf16[16,1,16,256]{3,2,1,0:T(8,128)(2,1)S(1)}, u32[]{:S(2)}, u32[]{:S(2)}) async-start(bf16[16,1,16,256]{3,2,1,0:T(8,128)(2,1)} %bitcast.4), calls=%async_computation | async-start | bytes 262144 | tf_op jit(solution)/shard_map/all_to_all | solution.py:137
  110.1 3.8 %while.35 = (s32[]{:T(128)}, f32[16,256]{1,0:T(8,128)S(1)}, f32[256,256]{1,0:T(8,128)S(1)}, f32[4,16,512]{2,1,0:T(8,128)S(1)}, bf16[4,512,256]{2,1,0:T(8,128)(2,...) while((s32[]{:T(128)}, f32[16,256]{1,0:T(8,128)S(1)}, f32[256,256]{1,0:T(8,128)S(1)}, ...), condition=%wide.region_11.13_spmd.clone, body=%wide.region_10.12_spmd.clone.sunk | while | flops 428220416 | bytes 1384576 | solution.py:116
  116.9 1.5 all-to-all-done
  118.6 4.0 %while.36 = (s32[]{:T(128)}, f32[256,256]{1,0:T(8,128)S(1)}, s32[2,2]{1,0:T(2,128)S(1)}, f32[2,128,128]{2,1,0:T(8,128)S(1)}, s32[]{:T(128)}) while((s32[]{:T(128)}, f32[256,256]{1,0:T(8,128)S(1)}, s32[2,2]{1,0:T(2,128)S(1)}, f32[2,128,128]{2,1,0:T(8,128)S(1)}, s32[]{:T(128)}) %tuple.98), condition=%wide.while_cond, body=%wide.while_body.sunk | while | flops 2 | bytes 131181 | solution.py:64
  119.2 1.4 bitcast_dynamic-update-slice_fusion.4
  121.2 1.4 bitcast_dynamic-update-slice_fusion.4
  122.6 19.9 %custom-call.23 = f32[2,128,128]{1,2,0:T(8,128)S(1)} custom-call(f32[2,128,128]{2,1,0:T(8,128)S(1)} %get-tuple-element.199), custom_call_target="InvertDiagBlocksLowerTriangular" | custom-call | tf_op jit(solution)/shard_map/while/body/eval_jaxpr/triangular_solve/custom-call.0 | solution.py:64
  144.1 1.1 fusion.16
  145.4 11.7 %cholesky.49 = f32[128,128]{1,0:T(8,128)S(1)} custom-call(f32[128,128]{1,0:T(8,128)S(1)} %cholesky.115), custom_call_target="Cholesky" | custom-call | tf_op jit(solution)/shard_map/while/body/eval_jaxpr/jit(cholesky)/cholesky | solution.py:68
  157.1 9.8 %custom-call.17 = f32[1,128,128]{1,2,0:T(8,128)S(1)} custom-call(f32[1,128,128]{2,1,0:T(8,128)S(1)} %get-tuple-element.292), custom_call_target="InvertDiagBlocksLowerTriangular" | custom-call | tf_op jit(solution)/shard_map/while/body/eval_jaxpr/jit(cholesky)/cholesky | solution.py:68
  167.4 11.7 %cholesky.103 = f32[128,128]{1,0:T(8,128)S(1)} custom-call(f32[128,128]{1,0:T(8,128)S(1)} %convolution_subtract_fusion.2), custom_call_target="Cholesky" | custom-call | tf_op jit(solution)/shard_map/while/body/eval_jaxpr/jit(cholesky)/cholesky | solution.py:68
  182.3 4.3 %while.37 = (s32[]{:T(128)}, f32[256,256]{0,1:T(8,128)S(1)}, s32[2,2]{1,0:T(2,128)S(1)}, f32[2,128,128]{2,1,0:T(8,128)S(1)}, s32[]{:T(128)}) while((s32[]{:T(128)}, f32[256,256]{0,1:T(8,128)S(1)}, s32[2,2]{1,0:T(2,128)S(1)}, f32[2,128,128]{2,1,0:T(8,128)S(1)}, s32[]{:T(128)}) %tuple.112), condition=%wide.while_cond.clone, body=%wide.while_body.clone.sunk | while | flops 2 | bytes 393321 | solution.py:69
  182.9 1.4 dynamic-slice.21
  185.1 1.4 dynamic-slice.21
  186.6 19.9 %custom-call.24 = f32[2,128,128]{1,2,0:T(8,128)S(1)} custom-call(f32[2,128,128]{2,1,0:T(8,128)S(1)} %get-tuple-element.200), custom_call_target="InvertDiagBlocksLowerTriangular" | custom-call | tf_op jit(solution)/shard_map/while/body/eval_jaxpr/triangular_solve/custom-call.0 | solution.py:69
  217.3 7.2 %all-to-all-start.6 = ((f32[16,1,1,16,256]{4,3,2,1,0:T(8,128)}), f32[16,1,1,16,256]{4,3,2,1,0:T(8,128)S(1)}, u32[]{:S(2)}, u32[]{:S(2)}) async-start(f32[16,1,1,16,256]{4,3,2,1,0:T(8,128)} %constant_dynamic-update-slice_fusion), calls=%async_computation.6 | async-start | bytes 524288 | tf_op jit(solution)/shard_map/all_to_all | solution.py:147
  225.0 9.2 %all-to-all-done.6 = f32[16,1,1,16,256]{4,3,2,1,0:T(8,128)S(1)} async-done(((f32[16,1,1,16,256]{4,3,2,1,0:T(8,128)}), f32[16,1,1,16,256]{4,3,2,1,0:T(8,128)S(1)}, u32[]{:S(2)}, u32[]{:S(2)}) %all-to-all-start.6) | async-done | bytes 262176 | tf_op jit(solution)/shard_map/all_to_all | solution.py:147
  (118 shorter events, 28.8 us)
Async XLA Ops:
  2.6 39.1 %all-to-all-start.1 = ((bf16[16,128,256]{2,1,0:T(8,128)(2,1)}), bf16[16,128,256]{2,1,0:T(8,128)(2,1)S(1)}, u32[]{:S(2)}, u32[]{:S(2)}) async-start(bf16[16,128,256]{2,1,0:T(8,128)(2,1)} %broadcast_in_dim.32), calls=%async_computation.1 | async-start | bytes 2097152 | tf_op jit(solution)/shard_map/all_to_all | solution.py:16
  15.5 0.7 copy-start
  47.7 4.5 %copy-start.3 = (f32[16]{0:T(128)S(1)}, f32[16]{0:T(128)}, u32[]{:S(2)}) copy-start(f32[16]{0:T(128)} %param.13) | copy-start | bytes 196
  47.7 13.0 %all-to-all-start.2 = ((f32[16,16,128]{2,1,0:T(8,128)}), f32[16,16,128]{2,1,0:T(8,128)S(1)}, u32[]{:S(2)}, u32[]{:S(2)}) async-start(f32[16,16,128]{2,1,0:T(8,128)} %copy.56), calls=%async_computation.2 | async-start | bytes 262144 | tf_op jit(solution)/shard_map/all_to_all | solution.py:47
  93.1 12.6 %all-to-all-start.5 = ((f32[16,16,128]{2,1,0:T(8,128)}), f32[16,16,128]{2,1,0:T(8,128)S(1)}, u32[]{:S(2)}, u32[]{:S(2)}) async-start(f32[16,16,128]{2,1,0:T(8,128)} %broadcast_in_dim.35), calls=%async_computation.5 | async-start | bytes 262144 | tf_op jit(solution)/shard_map/all_to_all | solution.py:16
  105.7 12.7 %all-to-all-start = ((bf16[16,1,16,256]{3,2,1,0:T(8,128)(2,1)}), bf16[16,1,16,256]{3,2,1,0:T(8,128)(2,1)S(1)}, u32[]{:S(2)}, u32[]{:S(2)}) async-start(bf16[16,1,16,256]{3,2,1,0:T(8,128)(2,1)} %bitcast.4), calls=%async_computation | async-start | bytes 262144 | tf_op jit(solution)/shard_map/all_to_all | solution.py:137
  114.2 2.7 %copy-start.2 = (f32[16]{0:T(128)}, f32[16]{0:T(128)S(1)}, u32[]{:S(2)}) copy-start(f32[16]{0:T(128)S(1)} %get-tuple-element.512) | copy-start | bytes 196
  116.9 1.6 copy-start.1
  217.3 16.9 %all-to-all-start.6 = ((f32[16,1,1,16,256]{4,3,2,1,0:T(8,128)}), f32[16,1,1,16,256]{4,3,2,1,0:T(8,128)S(1)}, u32[]{:S(2)}, u32[]{:S(2)}) async-start(f32[16,1,1,16,256]{4,3,2,1,0:T(8,128)} %constant_dynamic-update-slice_fusion), calls=%async_computation.6 | async-start | bytes 524288 | tf_op jit(solution)/shard_map/all_to_all | solution.py:147
